TPU v7x, 256 devices: a whole 4x4x8 slice. The times are simulated.
256 devices in a mesh: dp: 64 (over z, y, core), mp: 4 (over x).
Axes of the slice: x: 4, y: 4, z: 8, core: 2. Of those that a mesh axis runs over, the one named last changes fastest.
Arguments:
- pixels: bfloat16 [1024, 256, 768], P('dp', 'mp'), may hold values from -6 to 6
- selection: int32 [1024], P('dp'), may hold values from 0 to 1, as said below
- destination: int32 [1024], P('dp'), may hold values from 0 to 63, as said below
- patch_weight: bfloat16 [768, 1024], replicated, may hold values from -0.21875 to 0.21875
- position: bfloat16 [256, 1024], P('mp'), may hold values from -6 to 6
- query_key_value: bfloat16 [3, 1024, 1024], P(None, None, 'mp'), may hold values from -1 to 1
- output_weight: bfloat16 [1024, 1024], P('mp'), may hold values from -0.1875 to 0.1875
- up_weight: bfloat16 [1024, 4096], P(None, 'mp'), may hold values from -0.1875 to 0.1875
- down_weight: bfloat16 [4096, 1024], P('mp'), may hold values from -0.09375 to 0.09375
- norm_gains: float32 [3, 1024], replicated, may hold values from 0.25 to 1.75
- embedding_weight: bfloat16 [1024, 1024], replicated, may hold values from -0.1875 to 0.1875
- caption_vectors: bfloat16 [1024, 1024], P('dp'), may hold values from -6 to 6
- loss_params: float32 [2], replicated, may hold values from -1 to 1
Outputs:
- image_embedding: float32 [256, 1024], P('dp')
- pair_loss: float32 [256], P('dp')
Inputs may be any that keep to these rules, and one draw needn't show every extreme that they name: `selection`: exactly 128 examples are selected in all; each index of dp holds between 1 and 3 of them, and some holds exactly 3. Among selected examples, at most 4 have the same destination, some destination has exactly 4, and no index of dp holds two selected examples with the same destination. Destinations of unselected examples are arbitrary.
All inputs are finite; a program needn't handle non-finite values.
Results may differ from a plain program's by a relative error of at most 0.0031.
Values may be sent and summed in bfloat16 or wider, within the bound.
A program may use at most 128 MiB of HBM per device.

v0:
```python
import jax
import jax.numpy as jnp
from jax import lax
from jax.sharding import PartitionSpec as P

HEAD_DIM = 64
PATCHES = 256
SEL_DEV = 2
SEND_MOST = 3
RECV_MOST = 4
EPS = 1e-06


def layer_norm(values, gain):
    center = jnp.mean(values, axis=-1, keepdims=True)
    centred = values - center
    spread = jnp.mean(centred * centred, axis=-1, keepdims=True)
    return centred * lax.rsqrt(spread + EPS) * gain


def unit_rows(values):
    scale = lax.rsqrt(jnp.mean(values * values, axis=-1, keepdims=True) + EPS)
    return values * scale * values.shape[-1] ** (-0.5)


def per_device(
    pixels,
    selection,
    destination,
    patch_weight,
    position,
    query_key_value,
    output_weight,
    up_weight,
    down_weight,
    norm_gains,
    embedding_weight,
    caption_vectors,
    loss_params,
):
    n_dp = lax.axis_size("dp")
    f32, bf16 = (jnp.float32, jnp.bfloat16)
    chosen = selection > 0
    local_rank = jnp.cumsum(selection) - 1
    picker = chosen[None, :] & (
        local_rank[None, :] == jnp.arange(SEND_MOST, dtype=jnp.int32)[:, None]
    )
    live = jnp.any(picker, axis=1)
    dest = jnp.sum(jnp.where(picker, destination[None, :] + 1, 0), axis=1) - 1
    index = jnp.sum(
        jnp.where(picker, jnp.arange(selection.shape[0], dtype=jnp.int32)[None, :], 0), axis=1
    )
    captions = jnp.dot(picker.astype(bf16), caption_vectors, preferred_element_type=f32).astype(
        bf16
    )
    all_captions = lax.all_gather(captions, "dp", axis=0, tiled=True)
    all_dest = lax.all_gather(dest, "dp", axis=0, tiled=True)
    image = jnp.stack(
        [lax.dynamic_index_in_dim(pixels, index[k], 0, keepdims=False) for k in range(SEND_MOST)]
    )
    image = lax.all_gather(image, "mp", axis=1, tiled=True)
    place = lax.all_gather(position, "mp", axis=0, tiled=True)
    output_all = lax.all_gather(output_weight, "mp", axis=0, tiled=True)
    hidden = (
        jnp.einsum("rpc,cd->rpd", image, patch_weight, preferred_element_type=f32)
        + place.astype(f32)[None]
    )
    normed = layer_norm(hidden, norm_gains[0]).astype(bf16)
    projected = jnp.einsum(
        "rpd,tdk->trpk", normed, query_key_value, preferred_element_type=f32
    ).astype(bf16)
    heads = projected.shape[-1] // HEAD_DIM
    shaped = projected.reshape(3, SEND_MOST, PATCHES, heads, HEAD_DIM)
    scores = jnp.einsum(
        "rqhd,rkhd->rhqk", shaped[0], shaped[1], preferred_element_type=f32
    ) * HEAD_DIM ** (-0.5)
    weights = jax.nn.softmax(scores, axis=-1).astype(bf16)
    context = jnp.einsum("rhqk,rkhd->rqhd", weights, shaped[2], preferred_element_type=f32).astype(
        bf16
    )
    context = context.reshape(SEND_MOST, PATCHES, heads * HEAD_DIM)
    context = lax.all_gather(context, "mp", axis=0)
    segments = output_all.reshape(lax.axis_size("mp"), -1, output_all.shape[-1])
    hidden = hidden + jnp.einsum("mrpk,mkd->rpd", context, segments, preferred_element_type=f32)
    normed = layer_norm(hidden, norm_gains[1]).astype(bf16)
    expanded = jax.nn.gelu(
        jnp.einsum("rpd,df->rpf", normed, up_weight, preferred_element_type=f32)
    ).astype(bf16)
    summed = jnp.sum(expanded.astype(f32), axis=1)
    part = jnp.dot(summed, down_weight.astype(f32), precision=lax.Precision.HIGHEST)
    rows = PATCHES // lax.axis_size("mp")
    own = lax.dynamic_slice_in_dim(hidden, lax.axis_index("mp") * rows, rows, axis=1)
    part = part + jnp.sum(own, axis=1)
    pooled = jnp.sum(lax.all_gather(part, "mp", axis=0), axis=0) / PATCHES
    normed = layer_norm(pooled, norm_gains[2]).astype(bf16)
    sorter = (dest[None, :] == jnp.arange(n_dp, dtype=jnp.int32)[:, None]) & live[None, :]
    outgoing = jnp.dot(sorter.astype(bf16), normed, preferred_element_type=f32).astype(bf16)
    arrived = lax.all_to_all(outgoing, "dp", split_axis=0, concat_axis=0, tiled=True)
    match = (all_dest == lax.axis_index("dp")).astype(jnp.int32).reshape(n_dp, SEND_MOST)
    present = jnp.sum(match, axis=1)
    place_of = jnp.cumsum(present) - present
    pick = (present[None, :] > 0) & (
        place_of[None, :] == jnp.arange(RECV_MOST, dtype=jnp.int32)[:, None]
    )
    filled = jnp.any(pick, axis=1)
    slots = jnp.dot(pick.astype(bf16), arrived, preferred_element_type=f32).astype(bf16)
    embedded = jnp.dot(slots, embedding_weight, preferred_element_type=f32)
    embedded = jnp.where(filled[:, None], embedded, 0.0)
    scale = 10.0 * jnp.exp(loss_params[0])
    shift = 2.0 * loss_params[1]
    logits = (
        scale
        * jnp.dot(
            unit_rows(embedded),
            unit_rows(all_captions.astype(f32)).T,
            precision=lax.Precision.HIGHEST,
        )
        + shift
    )
    same = (pick[:, :, None] & (match[None] > 0)).reshape(RECV_MOST, n_dp * SEND_MOST)
    signs = jnp.where(same, 1.0, -1.0)
    terms = jax.nn.softplus(-signs * logits) * (all_dest >= 0).astype(f32)[None, :]
    losses = jnp.where(filled, jnp.sum(terms, axis=1) / float(n_dp * SEL_DEV), 0.0)
    return (embedded, losses)


def solution(mesh):
    in_specs = (
        P("dp", "mp", None),
        P("dp"),
        P("dp"),
        P(),
        P("mp", None),
        P(None, None, "mp"),
        P("mp", None),
        P(None, "mp"),
        P("mp", None),
        P(),
        P(),
        P("dp", None),
        P(),
    )
    out_specs = (P("dp", None), P("dp"))
    return jax.shard_map(
        per_device, mesh=mesh, in_specs=in_specs, out_specs=out_specs, check_vma=False
    )
```

profile of v0, /device:TPU:1, one launch (start us, length us, event | category | flops | bytes accessed | tf_op | source)
XLA Modules:
  0.0 188.1 jit_solution(4609021758718230492)
XLA Ops:
  7.2 0.8 broadcast_compare_fusion.2
  8.0 0.7 copy.37
  8.8 0.1 add_reduce_fusion.1
  8.9 0.7 broadcast_add_fusion.1
  9.6 0.1 fusion.85
  9.7 0.1 select_reduce_fusion
  9.8 0.7 fusion.90
  16.5 1.0 constant_dynamic-slice_fusion.2
  17.5 0.8 pad_maximum_fusion
  18.3 0.7 all-gather.11.cloned.1.call-update
  19.1 12.5 %all_gather.26 = bf16[256,1024]{1,0:T(8,128)(2,1)S(1)} all-gather(bf16[64,1024]{1,0:T(8,128)(2,1)} %param.17), channel_id=1, replica_groups=mesh['dp'=64,'mp'=4] {'mp'}, dimensions={0}, use_global_device_ids=true | all-gather | bytes 655360 | tf_op jit(solution)/shard_map/all_gather | solution.py:62
  31.7 15.3 %all-gather.7.cloned.1.call-done = bf16[3,256,768]{2,1,0:T(8,128)(2,1)} async-done(((bf16[3,64,768]{2,1,0:T(8,128)(2,1)}), bf16[3,256,768]{2,1,0:T(8,128)(2,1)}) %all-gather.7.cloned.1.call-update) | async-done | bytes 1179664 | tf_op jit(solution)/shard_map/all_gather | solution.py:61
  47.0 3.3 %add_reduce_fusion = (f32[3,256]{1,0:T(4,128)S(1)}, f32[3,256,1024]{2,1,0:T(8,128)S(1)}) fusion(f32[256,1024]{1,0:T(8,128)S(1)} %convert_element_type.56, bf16[3,256,768]{2,1,0:T(8,128)(2,1)} %all-gather.7.cloned.1.call-done, bf16[768,1024]{1,0:T(8,128)(2,1)} %param.16), kind=kOutput, calls=%fused_computation.20 | convolution fusion | flops 1209531648 | bytes 6949888 | tf_op jit(solution)/shard_map/rpc,cd->rpd/dot_general | solution.py:65
  50.3 0.6 multiply_reduce_fusion.1
  51.0 1.9 copy-done.9
  52.8 2.1 %fusion.36 = bf16[3,3,256,256]{2,3,0,1:T(8,128)(2,1)S(1)} fusion(bf16[3,1024,256]{2,1,0:T(8,128)(2,1)S(1)} %copy-done.9, f32[3,256,1024]{2,1,0:T(8,128)S(1)} %get-tuple-element.28, f32[1024]{0:T(1024)S(1)} %bitcast.85, f32[3,256]{1,0:T(4,128)S(1)} %add_rsqrt_fusion.1, f32[3,256]{1,0:T(4,128)S(1)} %broadcast_multiply_fusion.1, ...), kind=kOutput, calls=%fused_computation.38 | convolution fusion | flops 1212481536 | bytes 6957056 | tf_op jit(solution)/shard_map/rpd,tdk->trpk/dot_general | solution.py:69
  55.0 2.9 %fusion.91 = (f32[3,4,256]{2,1,0:T(4,128)S(1)}, f32[3,4,256,256]{2,3,1,0:T(8,128)}) fusion(bf16[3,256,4,64]{1,3,2,0:T(8,128)(2,1)S(1)} %bitcast.81, bf16[3,256,4,64]{1,3,2,0:T(8,128)(2,1)S(1)} %bitcast.80), kind=kOutput, calls=%fused_computation.116 | convolution fusion | flops 103022848 | bytes 3944448 | tf_op jit(solution)/shard_map/sub | solution.py:77
  57.9 2.3 %fusion.41 = bf16[3,4,64,256]{3,2,1,0:T(8,128)(2,1)S(1)} fusion(bf16[3,256,4,64]{1,3,2,0:T(8,128)(2,1)S(1)} %bitcast.79, f32[3,4,256,256]{2,3,1,0:T(8,128)} %get-tuple-element.30, f32[3,4,256]{2,1,0:T(4,128)S(1)} %get-tuple-element.29), kind=kOutput, calls=%fused_computation.39 | convolution fusion | flops 102432768 | bytes 3944448 | tf_op jit(solution)/shard_map/rhqk,rkhd->rqhd/dot_general | solution.py:78
  60.2 0.9 copy.41
  61.2 0.6 dynamic-slice
  62.5 20.4 %all-reduce = s32[192]{0:T(256)S(1)} all-reduce(s32[192]{0:T(256)S(1)} %get-tuple-element.26), channel_id=1, replica_groups=mesh['dp'=64,'mp'=4] {'dp'}, use_global_device_ids=true, to_apply=%add | all-reduce | flops 192 | bytes 1536
  82.9 0.1 reshape.193
  83.1 0.1 reduce_sum.145
  83.4 0.1 reduce.2
  83.5 0.1 fusion.44
  83.6 52.1 %all-gather.2 = bf16[64,3,1024]{2,1,0:T(4,128)(2,1)S(1)} all-gather(bf16[1,3,1024]{2,1,0:T(4,128)(2,1)S(1)} %fusion.44), channel_id=1, replica_groups=mesh['dp'=64,'mp'=4] {'dp'}, dimensions={0}, use_global_device_ids=true | all-gather | bytes 399360 | tf_op jit(solution)/shard_map/all_gather | solution.py:56
  135.7 0.3 reshape.205
  136.0 0.1 multiply_reduce_fusion.3
  136.1 0.1 fusion.83
  136.3 5.1 %fusion.92 = (f32[3,256]{1,0:T(4,128)S(1)}, f32[3,256,1024]{2,1,0:T(8,128)S(1)}) fusion(bf16[4,3,256,256]{3,2,0,1:T(8,128)(2,1)} %all-gather.9.cloned.1.call-done, bf16[4,256,1024,1]{2,1,0,3:T(8,128)(2,1)} %bitcast.88, f32[3,256,1024]{2,1,0:T(8,128)} %copy-done.2, f32[256,1024]{1,0:T(8,128)} %copy-done.1), kind=kOutput, calls=%fused_computation.117 | convolution fusion | flops 1612971264 | bytes 11013120 | tf_op jit(solution)/shard_map/mrpk,mkd->rpd/dot_general | solution.py:84
  141.4 0.5 multiply_reduce_fusion
  142.0 1.0 copy-done.8
  143.0 2.8 %convert_reduce_fusion = f32[3,1024]{1,0:T(4,128)S(1)} fusion(bf16[1024,1024]{1,0:T(8,128)(2,1)S(1)} %copy-done.8, f32[3,256,1024]{2,1,0:T(8,128)S(1)} %get-tuple-element.32, f32[1024]{0:T(1024)S(1)} %bitcast.84, f32[3,256]{1,0:T(4,128)S(1)} %add_rsqrt_fusion, f32[3,256]{1,0:T(4,128)S(1)} %broadcast_multiply_fusion), kind=kOutput, calls=%fused_computation.11 | convolution fusion | flops 1622406144 | bytes 5265408 | tf_op jit(solution)/shard_map/rpd,df->rpf/dot_general | solution.py:87
  145.8 0.9 fusion.43
  146.8 9.0 %all-gather.1 = f32[4,3,1024]{2,1,0:T(4,128)S(1)} all-gather(f32[1,3,1024]{2,1,0:T(4,128)S(1)} %fusion.43), channel_id=2, replica_groups=mesh['dp'=64,'mp'=4] {'mp'}, dimensions={0}, use_global_device_ids=true | all-gather | bytes 61440 | tf_op jit(solution)/shard_map/all_gather | solution.py:94
  155.8 0.1 multiply_reduce_fusion.6
  155.9 0.2 multiply_reduce_fusion.5
  156.1 0.2 fusion.42
  156.3 0.5 broadcast.192
  156.9 0.7 reduce.4
  157.5 0.7 reshape.217
  158.2 10.0 %all-to-all-start = ((bf16[64,2,512]{2,1,0:T(2,128)(2,1)}), bf16[64,2,512]{2,1,0:T(2,128)(2,1)S(1)}, u32[]{:S(2)}, u32[]{:S(2)}) async-start(bf16[64,2,512]{2,1,0:T(2,128)(2,1)} %reshape.217), calls=%async_computation | async-start | bytes 262144 | tf_op jit(solution)/shard_map/all_to_all | solution.py:98
  168.3 0.6 fusion.89
  169.0 0.2 and.53
  170.5 8.9 %all-to-all-done = bf16[64,2,512]{2,1,0:T(2,128)(2,1)S(1)} async-done(((bf16[64,2,512]{2,1,0:T(2,128)(2,1)}), bf16[64,2,512]{2,1,0:T(2,128)(2,1)S(1)}, u32[]{:S(2)}, u32[]{:S(2)}) %all-to-all-start) | async-done | bytes 131104 | tf_op jit(solution)/shard_map/all_to_all | solution.py:98
  179.5 0.6 multiply_reduce_fusion.4
  180.1 0.9 fusion.72
  181.1 0.5 multiply_select_fusion
  (50 shorter events, 1.1 us)
Async XLA Ops:
  7.2 172.3 %copy-start = (bf16[1024,1024]{1,0:T(8,128)(2,1)S(1)}, bf16[1024,1024]{1,0:T(8,128)(2,1)}, u32[]{:S(2)}) copy-start(bf16[1024,1024]{1,0:T(8,128)(2,1)} %param.23) | copy-start | bytes 6291460
  7.2 24.5 %copy-start.6 = (f32[3,1024]{1,0:T(4,128)S(1)}, f32[3,1024]{1,0:T(4,128)}, u32[]{:S(2)}) copy-start(f32[3,1024]{1,0:T(4,128)} %param.22) | copy-start | bytes 36868
  7.2 39.8 %all-gather.7.cloned.1.call-start = ((), (), s32[]{:S(2)}) async-start(), calls=%async_computation.1 | async-start | bytes 1474560 | tf_op jit(solution)/shard_map/all_gather | solution.py:61
  18.3 118.0 %all-gather.11.cloned.1.call-start = ((), (), s32[]{:S(2)}) async-start(), calls=%async_computation.3 | async-start | bytes 2621440 | tf_op jit(solution)/shard_map/all_gather | solution.py:63
  19.0 117.3 %all-gather.9.cloned.1.call-start = ((), (), s32[]{:S(2)}) async-start(), calls=%async_computation.2 | async-start | bytes 1966080 | tf_op jit(solution)/shard_map/all_gather | solution.py:82
  31.7 19.3 %copy-start.1 = (f32[256,1024]{1,0:T(8,128)}, f32[256,1024]{1,0:T(8,128)S(1)}, u32[]{:S(2)}) copy-start(f32[256,1024]{1,0:T(8,128)S(1)} %convert_element_type.56) | copy-start | bytes 3145732
  50.3 4.6 %copy-start.2 = (f32[3,256,1024]{2,1,0:T(8,128)}, f32[3,256,1024]{2,1,0:T(8,128)S(1)}, u32[]{:S(2)}) copy-start(f32[3,256,1024]{2,1,0:T(8,128)S(1)} %get-tuple-element.28) | copy-start | bytes 9437188
  50.3 2.5 %copy-start.9 = (bf16[3,1024,256]{2,1,0:T(8,128)(2,1)S(1)}, bf16[3,1024,256]{2,1,0:T(8,128)(2,1)}, u32[]{:S(2)}) copy-start(bf16[3,1024,256]{2,1,0:T(8,128)(2,1)} %param.18) | copy-start | bytes 4718596
  57.9 3.3 %copy-start.10 = (u32[256]{0:T(256)S(1)}, u32[256]{0:T(256)}, u32[]{:S(2)}) copy-start(u32[256]{0:T(256)} %constant.102) | copy-start | bytes 3076
  57.9 25.6 %copy-start.5 = (bf16[16,1024]{1,0:T(8,128)(2,1)S(1)}, bf16[16,1024]{1,0:T(8,128)(2,1)}, u32[]{:S(2)}) copy-start(bf16[16,1024]{1,0:T(8,128)(2,1)} %param.24) | copy-start | bytes 98308
  141.4 1.6 copy-start.8
  143.0 2.8 %copy-start.3 = (bf16[1024,1024]{1,0:T(8,128)(2,1)S(1)}, bf16[1024,1024]{1,0:T(8,128)(2,1)}, u32[]{:S(2)}) copy-start(bf16[1024,1024]{1,0:T(8,128)(2,1)} %param.21) | copy-start | bytes 6291460
  145.8 22.5 %copy-start.7 = (f32[2]{0:T(128)S(1)}, f32[2]{0:T(128)}, u32[]{:S(2)}) copy-start(f32[2]{0:T(128)} %param.25) | copy-start | bytes 28
  158.2 21.1 %all-to-all-start = ((bf16[64,2,512]{2,1,0:T(2,128)(2,1)}), bf16[64,2,512]{2,1,0:T(2,128)(2,1)S(1)}, u32[]{:S(2)}, u32[]{:S(2)}) async-start(bf16[64,2,512]{2,1,0:T(2,128)(2,1)} %reshape.217), calls=%async_computation | async-start | bytes 262144 | tf_op jit(solution)/shard_map/all_to_all | solution.py:98
  180.1 1.5 copy-start.4
Sparse Core Ops, SparseCore 0:
  18.4 28.5 all-gather.6
  48.8 35.8 all-gather.10
  86.5 29.0 all-gather.8
where the time goes:
time: 189 us; the launch traced here: 188 us
  blocking collectives  93.9 us (50%)
  waiting for transfers between devices  24.9 us (13%)
  between operations  22 us (12%)
  matrix products  21.3 us (11%)
  starting transfers between devices  10.2 us (5%)
  local copies, waits for them, and re-layouts  9.66 us (5%)
  other arithmetic  6.19 us (3%)
    all_gather x1, blocking collectives, per_device(): all_captions = lax.all_gather(captions, 'dp', axis=0, tiled=True)  52.1 us
    unnamed x1, blocking collectives  20.4 us
    all_gather x1, waiting for transfers between devices, per_device(): image = lax.all_gather(image, 'mp', axis=1, tiled=True)  15.3 us
    all_gather x1, blocking collectives, per_device(): place = lax.all_gather(position, 'mp', axis=0, tiled=True)  12.5 us
    all_to_all x1, starting transfers between devices, per_device(): lax.all_to_all(outgoing, 'dp', split_axis=0, concat_axis=0, tiled=True)  10 us
    all_gather x1, blocking collectives, per_device(): pooled = jnp.sum(lax.all_gather(part, 'mp', axis=0), axis=0) / PATCHES  8.97 us
    all_to_all x1, waiting for transfers between devices, per_device(): lax.all_to_all(outgoing, 'dp', split_axis=0, concat_axis=0, tiled=True)  8.89 us
    dot_general x1, matrix products, per_device(): jnp.einsum('mrpk,mkd->rpd', context, segments, preferred_element_type=f32)  5.1 us
  transfers between devices with their start and end apart: 4, of which 2 were waited for; matrix products, arithmetic and copies ran while one was open for 8% of the time, Pallas kernels for 0%

commit v1 on v0

--- a/solution.py
+++ b/solution.py
@@ -53,7 +53,9 @@
     captions = jnp.dot(picker.astype(bf16), caption_vectors, preferred_element_type=f32).astype(
         bf16
     )
-    all_captions = lax.all_gather(captions, "dp", axis=0, tiled=True)
+    all_captions = jnp.concatenate(
+        lax.all_to_all(jnp.stack([captions] * lax.axis_size("dp")), "dp", 0, 0), axis=0
+    )
     all_dest = lax.all_gather(dest, "dp", axis=0, tiled=True)
     image = jnp.stack(
         [lax.dynamic_index_in_dim(pixels, index[k], 0, keepdims=False) for k in range(SEND_MOST)]

time: 189 us -> 174 us (0.921)
  blocking collectives: 93.9 us -> 40.4 us
  waiting for transfers between devices: 24.9 us -> 43.3 us
  starting transfers between devices: 10.2 us -> 26.4 us
  other arithmetic: 6.19 us -> 8.09 us
    all_gather x1 -> x0, blocking collectives: 52.1 us -> none  [per_device(): all_captions = lax.all_gather(captions, 'dp', axis=0, tiled=True)]
    all_gather x1, waiting for transfers between devices: 0.02 us -> 17 us  [per_device(): context = lax.all_gather(context, 'mp', axis=0)]
    all_to_all x0 -> x1, starting transfers between devices: none -> 12.8 us  [per_device(): lax.all_to_all(jnp.stack([captions] * lax.axis_size('dp')), 'dp', 0, 0)]
    all_to_all x1, starting transfers between devices: 10 us -> 13.5 us  [per_device(): lax.all_to_all(outgoing, 'dp', split_axis=0, concat_axis=0, tiled=True)]
  transfers between devices with their start and end apart: 4 -> 5, of which waited for: 2 -> 3; matrix products, arithmetic and copies ran while one was open for 8% -> 17% of each run, Pallas kernels for 0% -> 0%
where the time goes in v1:
time: 174 us; the launch traced here: 173 us
  waiting for transfers between devices  43.3 us (25%)
  blocking collectives  40.4 us (23%)
  starting transfers between devices  26.4 us (15%)
  matrix products  22.3 us (13%)
  between operations  21.9 us (13%)
  local copies, waits for them, and re-layouts  10.8 us (6%)
  other arithmetic  8.09 us (5%)
    unnamed x1, blocking collectives  18.5 us
    all_gather x1, waiting for transfers between devices, per_device(): context = lax.all_gather(context, 'mp', axis=0)  17 us
    all_gather x1, waiting for transfers between devices, per_device(): image = lax.all_gather(image, 'mp', axis=1, tiled=True)  15.3 us
    all_to_all x1, starting transfers between devices, per_device(): lax.all_to_all(outgoing, 'dp', split_axis=0, concat_axis=0, tiled=True)  13.5 us
    all_to_all x1, starting transfers between devices, per_device(): lax.all_to_all(jnp.stack([captions] * lax.axis_size('dp')), 'dp', 0, 0)  12.8 us
    all_gather x1, blocking collectives, per_device(): place = lax.all_gather(position, 'mp', axis=0, tiled=True)  12.5 us
    all_to_all x1, waiting for transfers between devices, per_device(): lax.all_to_all(outgoing, 'dp', split_axis=0, concat_axis=0, tiled=True)  10.3 us
    all_gather x1, blocking collectives, per_device(): pooled = jnp.sum(lax.all_gather(part, 'mp', axis=0), axis=0) / PATCHES  9.42 us
  transfers between devices with their start and end apart: 5, of which 3 were waited for; matrix products, arithmetic and copies ran while one was open for 17% of the time, Pallas kernels for 0%

profile of v1, /device:TPU:1, one launch (start us, length us, event | category | flops | bytes accessed | tf_op | source)
XLA Modules:
  0.0 173.3 jit_solution(2042318819051753290)
XLA Ops:
  7.2 0.8 broadcast_compare_fusion.2
  8.0 0.7 copy.37
  8.9 0.7 broadcast_add_fusion.1
  9.7 0.1 select_reduce_fusion
  9.8 0.7 fusion.89
  16.5 1.0 constant_dynamic-slice_fusion.2
  17.5 0.8 pad_maximum_fusion
  18.3 0.7 all-gather.10.cloned.1.call-update
  19.1 12.5 %all_gather.23 = bf16[256,1024]{1,0:T(8,128)(2,1)S(1)} all-gather(bf16[64,1024]{1,0:T(8,128)(2,1)} %param.17), channel_id=1, replica_groups=mesh['dp'=64,'mp'=4] {'mp'}, dimensions={0}, use_global_device_ids=true | all-gather | bytes 655360 | tf_op jit(solution)/shard_map/all_gather | solution.py:64
  31.7 15.3 %all-gather.6.cloned.1.call-done = bf16[3,256,768]{2,1,0:T(8,128)(2,1)} async-done(((bf16[3,64,768]{2,1,0:T(8,128)(2,1)}), bf16[3,256,768]{2,1,0:T(8,128)(2,1)}) %all-gather.6.cloned.1.call-update) | async-done | bytes 1179664 | tf_op jit(solution)/shard_map/all_gather | solution.py:63
  47.0 3.2 %add_reduce_fusion = (f32[3,256]{1,0:T(4,128)S(1)}, f32[3,256,1024]{2,1,0:T(8,128)S(1)}) fusion(f32[256,1024]{1,0:T(8,128)S(1)} %convert_element_type.62, bf16[3,256,768]{2,1,0:T(8,128)(2,1)} %all-gather.6.cloned.1.call-done, bf16[768,1024]{1,0:T(8,128)(2,1)} %param.16), kind=kOutput, calls=%fused_computation.20 | convolution fusion | flops 1209531648 | bytes 6949888 | tf_op jit(solution)/shard_map/rpc,cd->rpd/dot_general | solution.py:67
  50.3 0.5 multiply_reduce_fusion.1
  50.8 2.0 %copy-done.9 = bf16[3,1024,256]{2,1,0:T(8,128)(2,1)S(1)} copy-done((bf16[3,1024,256]{2,1,0:T(8,128)(2,1)S(1)}, bf16[3,1024,256]{2,1,0:T(8,128)(2,1)}, u32[]{:S(2)}) %copy-start.9) | copy-done | bytes 1572888
  52.8 1.8 %fusion.36 = bf16[3,3,256,256]{2,3,0,1:T(8,128)(2,1)S(1)} fusion(bf16[3,1024,256]{2,1,0:T(8,128)(2,1)S(1)} %copy-done.9, f32[3,256,1024]{2,1,0:T(8,128)S(1)} %get-tuple-element.28, f32[1024]{0:T(1024)S(1)} %bitcast.83, f32[3,256]{1,0:T(4,128)S(1)} %add_rsqrt_fusion.2, f32[3,256]{1,0:T(4,128)S(1)} %broadcast_multiply_fusion.1, ...), kind=kOutput, calls=%fused_computation.38 | convolution fusion | flops 1212481536 | bytes 6957056 | tf_op jit(solution)/shard_map/rpd,tdk->trpk/dot_general | solution.py:71
  54.7 2.9 %fusion.90 = (f32[3,4,256]{2,1,0:T(4,128)S(1)}, f32[3,4,256,256]{2,3,1,0:T(8,128)}) fusion(bf16[3,256,4,64]{1,3,2,0:T(8,128)(2,1)S(1)} %bitcast.79, bf16[3,256,4,64]{1,3,2,0:T(8,128)(2,1)S(1)} %bitcast.78), kind=kOutput, calls=%fused_computation.115 | convolution fusion | flops 103022848 | bytes 3944448 | tf_op jit(solution)/shard_map/sub | solution.py:79
  57.6 2.3 %fusion.41 = bf16[3,4,64,256]{3,2,1,0:T(8,128)(2,1)S(1)} fusion(bf16[3,256,4,64]{1,3,2,0:T(8,128)(2,1)S(1)} %bitcast.77, f32[3,4,256,256]{2,3,1,0:T(8,128)} %get-tuple-element.30, f32[3,4,256]{2,1,0:T(4,128)S(1)} %get-tuple-element.29), kind=kOutput, calls=%fused_computation.39 | convolution fusion | flops 102432768 | bytes 3944448 | tf_op jit(solution)/shard_map/rhqk,rkhd->rqhd/dot_general | solution.py:80
  59.9 0.9 copy.41
  60.9 0.1 convolution_convert_fusion.1
  61.0 1.0 stack.5
  61.9 12.8 %all-to-all-start.1 = ((bf16[64,3,1024]{2,1,0:T(4,128)(2,1)}), bf16[64,3,1024]{2,1,0:T(4,128)(2,1)S(1)}, u32[]{:S(2)}, u32[]{:S(2)}) async-start(bf16[64,3,1024]{2,1,0:T(4,128)(2,1)} %stack.5), calls=%async_computation.1 | async-start | bytes 1048576 | tf_op jit(solution)/shard_map/all_to_all | solution.py:57
  74.8 0.6 dynamic-slice
  76.1 18.5 %all-reduce = s32[192]{0:T(256)S(1)} all-reduce(s32[192]{0:T(256)S(1)} %get-tuple-element.26), channel_id=1, replica_groups=mesh['dp'=64,'mp'=4] {'dp'}, use_global_device_ids=true, to_apply=%add | all-reduce | flops 192 | bytes 1536
  94.6 0.5 broadcast_compare_fusion
  95.2 0.1 reshape.207
  95.8 0.7 fusion.82
  96.6 0.2 and.53
  96.7 0.6 fusion.88
  98.6 17.0 %all-gather.8.cloned.1.call-done = bf16[4,3,256,256]{3,2,0,1:T(8,128)(2,1)} async-done(((bf16[1,3,256,256]{3,2,0,1:T(8,128)(2,1)}), bf16[4,3,256,256]{3,2,0,1:T(8,128)(2,1)}) %all-gather.8.cloned.1.call-update) | async-done | bytes 1572880 | tf_op jit(solution)/shard_map/all_gather | solution.py:84
  115.6 5.1 %fusion.91 = (f32[3,256]{1,0:T(4,128)S(1)}, f32[3,256,1024]{2,1,0:T(8,128)S(1)}) fusion(bf16[4,3,256,256]{3,2,0,1:T(8,128)(2,1)} %all-gather.8.cloned.1.call-done, bf16[4,256,1024,1]{2,1,0,3:T(8,128)(2,1)} %bitcast.86, f32[3,256,1024]{2,1,0:T(8,128)} %copy-done.2, f32[256,1024]{1,0:T(8,128)} %copy-done.1), kind=kOutput, calls=%fused_computation.116 | convolution fusion | flops 1612971264 | bytes 11013120 | tf_op jit(solution)/shard_map/mrpk,mkd->rpd/dot_general | solution.py:86
  120.7 0.5 multiply_reduce_fusion
  121.3 1.0 copy-done.8
  122.3 2.8 %convert_reduce_fusion = f32[3,1024]{1,0:T(4,128)S(1)} fusion(bf16[1024,1024]{1,0:T(8,128)(2,1)S(1)} %copy-done.8, f32[3,256,1024]{2,1,0:T(8,128)S(1)} %get-tuple-element.32, f32[1024]{0:T(1024)S(1)} %bitcast.82, f32[3,256]{1,0:T(4,128)S(1)} %add_rsqrt_fusion.1, f32[3,256]{1,0:T(4,128)S(1)} %broadcast_multiply_fusion), kind=kOutput, calls=%fused_computation.11 | convolution fusion | flops 1622406144 | bytes 5265408 | tf_op jit(solution)/shard_map/rpd,df->rpf/dot_general | solution.py:89
  125.1 0.9 fusion.43
  126.0 9.4 %all-gather.1 = f32[4,3,1024]{2,1,0:T(4,128)S(1)} all-gather(f32[1,3,1024]{2,1,0:T(4,128)S(1)} %fusion.43), channel_id=2, replica_groups=mesh['dp'=64,'mp'=4] {'mp'}, dimensions={0}, use_global_device_ids=true | all-gather | bytes 61440 | tf_op jit(solution)/shard_map/all_gather | solution.py:96
  135.5 0.1 multiply_reduce_fusion.6
  135.6 0.2 multiply_reduce_fusion.5
  135.8 0.2 fusion.42
  136.0 0.5 broadcast.198
  136.6 0.7 reduce.5
  137.2 0.7 reshape.229
  138.0 13.5 %all-to-all-start = ((bf16[64,2,512]{2,1,0:T(2,128)(2,1)}), bf16[64,2,512]{2,1,0:T(2,128)(2,1)S(1)}, u32[]{:S(2)}, u32[]{:S(2)}) async-start(bf16[64,2,512]{2,1,0:T(2,128)(2,1)} %reshape.229), calls=%async_computation | async-start | bytes 262144 | tf_op jit(solution)/shard_map/all_to_all | solution.py:100
  151.4 0.3 multiply_reduce_fusion.3
  151.8 0.1 rsqrt.48
  151.9 0.3 reshape.211
  152.2 10.3 %all-to-all-done = bf16[64,2,512]{2,1,0:T(2,128)(2,1)S(1)} async-done(((bf16[64,2,512]{2,1,0:T(2,128)(2,1)}), bf16[64,2,512]{2,1,0:T(2,128)(2,1)S(1)}, u32[]{:S(2)}, u32[]{:S(2)}) %all-to-all-start) | async-done | bytes 131104 | tf_op jit(solution)/shard_map/all_to_all | solution.py:100
  162.7 1.3 multiply_reduce_fusion.4
  163.9 1.6 fusion.71
  165.5 1.2 multiply_select_fusion
  (53 shorter events, 1.6 us)
Async XLA Ops:
  7.2 155.5 %copy-start = (bf16[1024,1024]{1,0:T(8,128)(2,1)S(1)}, bf16[1024,1024]{1,0:T(8,128)(2,1)}, u32[]{:S(2)}) copy-start(bf16[1024,1024]{1,0:T(8,128)(2,1)} %param.23) | copy-start | bytes 6291460
  7.2 24.5 %copy-start.6 = (f32[3,1024]{1,0:T(4,128)S(1)}, f32[3,1024]{1,0:T(4,128)}, u32[]{:S(2)}) copy-start(f32[3,1024]{1,0:T(4,128)} %param.22) | copy-start | bytes 36868
  7.2 39.8 %all-gather.6.cloned.1.call-start = ((), (), s32[]{:S(2)}) async-start(), calls=%async_computation.2 | async-start | bytes 1474560 | tf_op jit(solution)/shard_map/all_gather | solution.py:63
  18.3 80.3 %all-gather.10.cloned.1.call-start = ((), (), s32[]{:S(2)}) async-start(), calls=%async_computation.4 | async-start | bytes 2621440 | tf_op jit(solution)/shard_map/all_gather | solution.py:65
  19.0 96.6 %all-gather.8.cloned.1.call-start = ((), (), s32[]{:S(2)}) async-start(), calls=%async_computation.3 | async-start | bytes 1966080 | tf_op jit(solution)/shard_map/all_gather | solution.py:84
  31.7 19.1 %copy-start.1 = (f32[256,1024]{1,0:T(8,128)}, f32[256,1024]{1,0:T(8,128)S(1)}, u32[]{:S(2)}) copy-start(f32[256,1024]{1,0:T(8,128)S(1)} %convert_element_type.62) | copy-start | bytes 3145732
  50.2 4.4 %copy-start.2 = (f32[3,256,1024]{2,1,0:T(8,128)}, f32[3,256,1024]{2,1,0:T(8,128)S(1)}, u32[]{:S(2)}) copy-start(f32[3,256,1024]{2,1,0:T(8,128)S(1)} %get-tuple-element.28) | copy-start | bytes 9437188
  50.2 2.5 %copy-start.9 = (bf16[3,1024,256]{2,1,0:T(8,128)(2,1)S(1)}, bf16[3,1024,256]{2,1,0:T(8,128)(2,1)}, u32[]{:S(2)}) copy-start(bf16[3,1024,256]{2,1,0:T(8,128)(2,1)} %param.18) | copy-start | bytes 4718596
  57.6 3.3 %copy-start.5 = (bf16[16,1024]{1,0:T(8,128)(2,1)S(1)}, bf16[16,1024]{1,0:T(8,128)(2,1)}, u32[]{:S(2)}) copy-start(bf16[16,1024]{1,0:T(8,128)(2,1)} %param.24) | copy-start | bytes 98308
  57.6 17.2 %copy-start.10 = (u32[256]{0:T(256)S(1)}, u32[256]{0:T(256)}, u32[]{:S(2)}) copy-start(u32[256]{0:T(256)} %constant.102) | copy-start | bytes 3076
  57.6 39.2 %copy-start.7 = (f32[2]{0:T(128)S(1)}, f32[2]{0:T(128)}, u32[]{:S(2)}) copy-start(f32[2]{0:T(128)} %param.25) | copy-start | bytes 28
  61.9 76.0 %all-to-all-start.1 = ((bf16[64,3,1024]{2,1,0:T(4,128)(2,1)}), bf16[64,3,1024]{2,1,0:T(4,128)(2,1)S(1)}, u32[]{:S(2)}, u32[]{:S(2)}) async-start(bf16[64,3,1024]{2,1,0:T(4,128)(2,1)} %stack.5), calls=%async_computation.1 | async-start | bytes 1048576 | tf_op jit(solution)/shard_map/all_to_all | solution.py:57
  120.7 1.6 copy-start.8
  122.3 2.8 %copy-start.3 = (bf16[1024,1024]{1,0:T(8,128)(2,1)S(1)}, bf16[1024,1024]{1,0:T(8,128)(2,1)}, u32[]{:S(2)}) copy-start(bf16[1024,1024]{1,0:T(8,128)(2,1)} %param.21) | copy-start | bytes 6291460
  138.0 24.6 %all-to-all-start = ((bf16[64,2,512]{2,1,0:T(2,128)(2,1)}), bf16[64,2,512]{2,1,0:T(2,128)(2,1)S(1)}, u32[]{:S(2)}, u32[]{:S(2)}) async-start(bf16[64,2,512]{2,1,0:T(2,128)(2,1)} %reshape.229), calls=%async_computation | async-start | bytes 262144 | tf_op jit(solution)/shard_map/all_to_all | solution.py:100
  163.9 2.8 %copy-start.4 = (f32[4,1024]{1,0:T(4,128)}, f32[4,1024]{1,0:T(4,128)S(1)}, u32[]{:S(2)}) copy-start(f32[4,1024]{1,0:T(4,128)S(1)} %get-tuple-element.34) | copy-start | bytes 49156
Sparse Core Ops, SparseCore 0:
  18.4 28.5 all-gather.5
  48.8 35.8 all-gather.9
  86.5 29.0 all-gather.7
